TPU v7x, 32 devices: a whole 2x2x4 slice. The times are simulated.
32 devices in a mesh: tm: 8 (over z, x), rows: 4 (over y, core).
Axes of the slice: x: 2, y: 2, z: 4, core: 2. Of those that a mesh axis runs over, the one named last changes fastest.
Arguments:
- initial_warmth: float32 [1024, 1024], P('rows'), may hold values from -6 to 6
- pattern_choice: int32 [16, 8, 8], P('tm'), may hold values from 0 to 7
- dissipation_tables: float32 [8, 128, 128], replicated, may hold values from -6 to 6
- material_label: int32 [8, 8], replicated, may hold values from 0 to 3
- intercept_kappa: float32 [4], replicated, may hold values from 4 to 8
- sensitivity_coef: float32 [4], replicated, may hold values from -0.5 to 0.5
Outputs:
- warmth_trajectory: float32 [16, 1024, 1024], P('tm', 'rows')
All inputs are finite; a program needn't handle non-finite values.
Results may differ from a plain program's by a relative error of at most 0.0003.
Values sent between devices are 32-bit elements; how exact they have to be, the bound alone decides.
A program may use at most 128 MiB of HBM per device.

v0:
```python
import math
import jax
import jax.numpy as jnp
from jax import lax
from jax.sharding import PartitionSpec as P

TILE = 128
ITERS = 2
TIMESTEP_SIZE = 2.0
ALPHA = 0.05
CROSS_WEIGHT = 1.0 / 64.0
HIGHEST = lax.Precision.HIGHEST


def extended(block, sides, width):
    for axis, dim in sides:
        count = lax.axis_size(axis)
        forward = [(i, i + 1) for i in range(count - 1)]
        backward = [(target, source) for source, target in forward]
        low = lax.ppermute(
            lax.slice_in_dim(block, block.shape[dim] - width, None, axis=dim), axis, forward
        )
        high = lax.ppermute(lax.slice_in_dim(block, 0, width, axis=dim), axis, backward)
        block = jnp.concatenate([low, block, high], axis=dim)
    return block


def shifted(block, axis, distance):
    devices = range(lax.axis_size(axis))
    route = [(i - distance, i) for i in devices if i - distance in devices]
    return lax.ppermute(block, axis, route)


def cosine_tables(length):
    modes = jnp.arange(length, dtype=jnp.int32)[:, None]
    cells = jnp.arange(length, dtype=jnp.int32)[None, :]
    phase = modes * (2 * cells + 1) % (4 * length)
    forward = jnp.cos(phase.astype(jnp.float32) * (math.pi / (2 * length)))
    weights = jnp.where(jnp.arange(length) == 0, 1.0, 2.0).astype(jnp.float32) / length
    inverse = forward.T * weights[None, :]
    return (forward, inverse)


def along_last(values, table):
    array_extent = values.shape
    flat = jnp.dot(
        values.reshape(-1, array_extent[-1]),
        table.T,
        precision=HIGHEST,
        preferred_element_type=jnp.float32,
    )
    return flat.reshape(array_extent[:-1] + (table.shape[0],))


def along_rows(values, table):
    return jnp.einsum("kn,afnc->afkc", table, values, precision=HIGHEST)


def fourier_forward(values):
    count = values.shape[0]
    index = jnp.arange(count, dtype=jnp.int32)
    phase = (index[:, None] * index[None, :] % count).astype(jnp.float32) * (2.0 * math.pi / count)
    table = jnp.concatenate([jnp.cos(phase), -jnp.sin(phase)], 0)
    flat = jnp.dot(
        table, values.reshape(count, -1), precision=HIGHEST, preferred_element_type=jnp.float32
    )
    return flat.reshape((2, count) + values.shape[1:])


def fourier_inverse(values):
    count = values.shape[1]
    index = jnp.arange(count, dtype=jnp.int32)
    phase = (index[:, None] * index[None, :] % count).astype(jnp.float32) * (2.0 * math.pi / count)
    table = jnp.concatenate([jnp.cos(phase), -jnp.sin(phase)], 1) / count
    flat = jnp.dot(
        table, values.reshape(2 * count, -1), precision=HIGHEST, preferred_element_type=jnp.float32
    )
    return flat.reshape((count,) + values.shape[2:])


def shifted_solve(spectra, freq_ids, column_ids, total_steps, grid_height, tile_pitch, conduct):
    shrink = ALPHA ** (1.0 / total_steps)
    theta = (freq_ids % total_steps).astype(jnp.float32) * (2.0 * math.pi / total_steps)
    mu_rows = 2.0 - 2.0 * jnp.cos(
        jnp.arange(grid_height).astype(jnp.float32) * (math.pi / grid_height)
    )
    mu_cols = 2.0 - 2.0 * jnp.cos(column_ids.astype(jnp.float32) * (math.pi / tile_pitch))
    real_den = (1.0 - shrink * jnp.cos(theta))[:, None, None] / TIMESTEP_SIZE + conduct * (
        mu_rows[None, :, None] + CROSS_WEIGHT * mu_cols[None, None, :]
    )
    imag_den = (shrink * jnp.sin(theta) / TIMESTEP_SIZE)[:, None, None]
    norm_den = real_den * real_den + imag_den * imag_den
    real_part = spectra[0]
    imag_part = spectra[1]
    solved_re = (real_part * real_den + imag_part * imag_den) / norm_den
    solved_im = (imag_part * real_den - real_part * imag_den) / norm_den
    return jnp.stack([solved_re, solved_im], 0)


def compute_residual(
    warmth_trajectory, initial_warmth, forcing_term, reference_grid, slope_grid, inner_boundaries
):
    extended_grid = extended(warmth_trajectory, (("rows", 1),), 1)
    kappa_local = reference_grid[None] * (1.0 + slope_grid[None] * jnp.tanh(extended_grid))
    upward_current = (
        0.5
        * (kappa_local[:, 1:] + kappa_local[:, :-1])
        * (extended_grid[:, 1:] - extended_grid[:, :-1])
    )
    upward_current = jnp.where(inner_boundaries[None, :, None], upward_current, 0.0)
    centre = extended_grid[:, 1:-1]
    kappa_mid = kappa_local[:, 1:-1]
    lateral_current = CROSS_WEIGHT * (
        0.5 * (kappa_mid[:, :, 1:] + kappa_mid[:, :, :-1]) * (centre[:, :, 1:] - centre[:, :, :-1])
    )
    zero_column = jnp.zeros_like(centre[:, :, :1])
    across = jnp.concatenate([lateral_current, zero_column], 2) - jnp.concatenate(
        [zero_column, lateral_current], 2
    )
    energy_ledger = upward_current[:, 1:] - upward_current[:, :-1] + across
    evolving_warmth = shifted(warmth_trajectory[-1], "tm", 1)
    evolving_warmth = jnp.where(lax.axis_index("tm") == 0, initial_warmth, evolving_warmth)
    former_warmth = jnp.concatenate([evolving_warmth[None], warmth_trajectory[:-1]], 0)
    return forcing_term - (warmth_trajectory - former_warmth) / TIMESTEP_SIZE + energy_ledger


def shards(
    initial_warmth,
    pattern_choice,
    dissipation_tables,
    material_label,
    intercept_kappa,
    sensitivity_coef,
):
    shard_moments = pattern_choice.shape[0]
    slab_tallies, tile_pitch = initial_warmth.shape
    tm_count = lax.axis_size("tm")
    rows_count = lax.axis_size("rows")
    total_steps = shard_moments * tm_count
    grid_height = slab_tallies * rows_count
    tiles_across = tile_pitch // TILE
    first_row = lax.axis_index("rows") * slab_tallies
    local_rows = first_row + jnp.arange(slab_tallies, dtype=jnp.int32)
    chosen = jnp.take(pattern_choice, local_rows // TILE, axis=1)
    pattern_rows = jnp.take(dissipation_tables, local_rows % TILE, axis=1)
    forcing_term = jnp.zeros((shard_moments, slab_tallies, tiles_across, TILE), jnp.float32)
    for pattern in range(dissipation_tables.shape[0]):
        forcing_term = forcing_term + jnp.where(
            (chosen == pattern)[..., None], pattern_rows[pattern][None, :, None, :], 0.0
        )
    forcing_term = forcing_term.reshape(shard_moments, slab_tallies, tile_pitch)
    padded_rows = first_row - 1 + jnp.arange(slab_tallies + 2, dtype=jnp.int32)
    labels = jnp.take(material_label, jnp.clip(padded_rows, 0, grid_height - 1) // TILE, axis=0)
    base_tiles = jnp.zeros(labels.shape, jnp.float32)
    slope_tiles = jnp.zeros(labels.shape, jnp.float32)
    for label in range(intercept_kappa.shape[0]):
        base_tiles = jnp.where(labels == label, intercept_kappa[label], base_tiles)
        slope_tiles = jnp.where(labels == label, sensitivity_coef[label], slope_tiles)
    reference_grid = jnp.repeat(base_tiles, TILE, axis=1)
    slope_grid = jnp.repeat(slope_tiles, TILE, axis=1)
    upper_rows = padded_rows[:-1]
    inner_boundaries = (upper_rows >= 0) & (upper_rows + 1 <= grid_height - 1)
    conduct = jnp.mean(intercept_kappa)
    step_ids = lax.axis_index("tm") * shard_moments + jnp.arange(shard_moments, dtype=jnp.int32)
    amplification = jnp.exp(step_ids.astype(jnp.float32) * (math.log(ALPHA) / total_steps))
    column_fwd, column_inv = cosine_tables(tile_pitch)
    row_fwd, row_inv = cosine_tables(grid_height)
    narrow = tile_pitch // (tm_count * rows_count)
    arrival = jnp.arange(tile_pitch, dtype=jnp.int32)
    strip_of = arrival // (tm_count * narrow)
    block_of = arrival // narrow % tm_count
    mode_order = block_of * (rows_count * narrow) + strip_of * narrow + arrival % narrow
    column_back = jnp.take(column_inv, mode_order, axis=1)
    warmth_trajectory = jnp.broadcast_to(
        initial_warmth[None], (shard_moments, slab_tallies, tile_pitch)
    )
    for sweep in range(ITERS):
        defect_vector = compute_residual(
            warmth_trajectory,
            initial_warmth,
            forcing_term,
            reference_grid,
            slope_grid,
            inner_boundaries,
        )
        scaled = defect_vector * amplification[:, None, None]
        column_modes = along_last(scaled, column_fwd)
        gathered = lax.all_to_all(
            lax.all_to_all(column_modes, "tm", split_axis=2, concat_axis=0, tiled=True),
            "rows",
            split_axis=2,
            concat_axis=1,
            tiled=True,
        )
        column_width = gathered.shape[2]
        column_ids = (
            lax.axis_index("tm") * (rows_count * column_width)
            + lax.axis_index("rows") * column_width
            + jnp.arange(column_width, dtype=jnp.int32)
        )
        spectra = along_rows(fourier_forward(gathered), row_fwd)
        freq_ids = jnp.arange(total_steps, dtype=jnp.int32)
        solved = shifted_solve(
            spectra, freq_ids, column_ids, total_steps, grid_height, tile_pitch, conduct
        )
        solved = along_rows(solved, row_inv)
        field = fourier_inverse(solved)
        correction_delta = lax.all_to_all(
            lax.all_to_all(field, "tm", split_axis=0, concat_axis=2, tiled=True),
            "rows",
            split_axis=1,
            concat_axis=2,
            tiled=True,
        )
        correction_delta = along_last(correction_delta, column_back)
        warmth_trajectory = warmth_trajectory + correction_delta / amplification[:, None, None]
    return warmth_trajectory


def solution(mesh):
    in_specs = (P("rows", None), P("tm", None, None), P(), P(), P(), P())
    out_specs = P("tm", "rows", None)
    return jax.shard_map(shards, mesh=mesh, in_specs=in_specs, out_specs=out_specs, check_vma=False)
```

profile of v0, /device:TPU:0, one launch (start us, length us, event | category | flops | bytes accessed | tf_op | source)
XLA Modules:
  0.0 817.1 jit_solution(5478636304248418031)
XLA Ops:
  0.0 6.0 collective-permute-start
  12.4 2.9 subtract_multiply_fusion
  15.9 2.4 gather_fusion.1
  31.0 2.1 broadcast_in_dim.320
  41.0 1.9 broadcast_in_dim.344
  43.0 2.2 broadcast_in_dim.345
  45.2 1.9 broadcast_in_dim.350
  47.2 2.2 broadcast_in_dim.351
  49.4 1.9 broadcast_in_dim.356
  51.3 2.2 broadcast_in_dim.357
  55.9 2.6 select_select_fusion.1
  58.6 2.7 select_select_fusion
  61.3 5.9 select_add_fusion
  75.1 26.0 %fusion.29 = f32[2,256,1024]{2,1,0:T(8,128)} fusion(f32[2,257,1024]{2,1,0:T(8,128)S(1)} %fusion.46, f32[2,256,1024]{2,1,0:T(8,128)S(1)} %copy-done.13, f32[1,256,1024]{2,1,0:T(8,128)S(1)} %bitcast.225, f32[1,256,1024]{2,1,0:T(8,128)S(1)} %select_bitcast_fusion.2, s32[1024]{0:T(1024)S(1)} %copy-done.15, f32[2,256,1023]{2,1,0:T(8,128)S(1)} %fusion.91, ...), kind=kOutput, calls=%fused_computation.44 | convolution fusion | flops 6461849600 | bytes 13636096 | tf_op jit(solution)/shard_map/dot_general | solution.py:46
  101.0 2.8 copy.60
  103.9 52.3 %all_to_all.132 = f32[2,256,1024]{1,0,2:T(2,128)S(1)} all-to-all(f32[2,256,1024]{1,0,2:T(2,128)S(1)} %copy.60), channel_id=1, replica_groups=mesh['tm'=8,'rows'=4] {'tm'}, dimensions={2} | all-to-all | bytes 4194304 | tf_op jit(solution)/shard_map/all_to_all | solution.py:189
  156.4 1.8 copy.62
  158.2 3.1 copy.63
  161.3 4.6 all-to-all-start.1
  167.6 23.9 %all-to-all-done.1 = f32[16,256,128]{1,0,2:T(8,128)S(1)} async-done(((f32[16,256,128]{1,0,2:T(8,128)}), f32[16,256,128]{1,0,2:T(8,128)S(1)}, u32[]{:S(2)}, u32[]{:S(2)}) %all-to-all-start.1) | async-done | bytes 2097184 | tf_op jit(solution)/shard_map/all_to_all | solution.py:188
  191.6 4.7 copy.65
  196.2 6.0 reshape.506
  202.2 4.8 dot_general.61
  207.1 5.5 copy.66
  212.5 3.4 fusion.109
  215.9 33.4 %fusion.53 = f32[2,16,1024,32]{2,3,1,0:T(8,128)S(1)} fusion(f32[2,16,1024,32]{2,1,3,0:T(8,128)S(1)} %fusion.109, s32[1024]{0:T(1024)S(1)} %copy-done.15), kind=kOutput, calls=%fused_computation.74 | convolution fusion | flops 12899581952 | bytes 8392704 | tf_op jit(solution)/shard_map/kn,afnc->afkc/dot_general | solution.py:56
  250.5 30.6 %fusion.68 = f32[2,16,1024,32]{2,3,1,0:T(8,128)} fusion(f32[1,16,1024,32]{2,3,1,0:T(8,128)S(1)} %get-tuple-element.13, f32[1,16,1024,32]{2,3,1,0:T(8,128)S(1)} %get-tuple-element.12, f32[1024]{0:T(1024)S(1)} %select_multiply_fusion, s32[1024]{0:T(1024)S(1)} %copy-done.15), kind=kOutput, calls=%fused_computation.77 | convolution fusion | flops 12901679104 | bytes 8396800 | tf_op jit(solution)/shard_map/kn,afnc->afkc/dot_general | solution.py:56
  281.2 10.4 %copy.69 = f32[2,16,1024,32]{3,2,1,0:T(8,128)} copy(f32[2,16,1024,32]{2,3,1,0:T(8,128)} %fusion.68) | data formatting | bytes 8388608 | tf_op jit(solution)/shard_map/kn,afnc->afkc/transpose | solution.py:56
  291.6 11.6 %reshape.507 = f32[32,32768]{1,0:T(8,128)} reshape(f32[2,16,1024,32]{3,2,1,0:T(8,128)} %copy.69) | data formatting | bytes 8388608 | tf_op jit(solution)/shard_map/reshape | solution.py:76
  303.3 9.8 %dot_general.66 = f32[1024,32,32]{1,0,2:T(8,128)} reshape(f32[32768,32]{0,1:T(8,128)} %bitcast.226) | data formatting | bytes 8388608 | tf_op jit(solution)/shard_map/dot_general | solution.py:75
  313.1 11.8 %copy.70 = f32[1024,32,32]{0,2,1:T(8,128)} copy(f32[1024,32,32]{1,0,2:T(8,128)} %dot_general.66) | data formatting | bytes 8388608 | tf_op jit(solution)/shard_map/dot_general | solution.py:75
  324.9 4.1 fusion.165
  330.3 51.1 %all_to_all.133 = f32[16,1024,32]{1,2,0:T(8,128)S(1)} all-to-all(f32[16,1024,32]{1,2,0:T(8,128)S(1)} %copy.71), channel_id=1, replica_groups=mesh['tm'=8,'rows'=4] {'tm'}, dimensions={0} | all-to-all | bytes 4194304 | tf_op jit(solution)/shard_map/all_to_all | solution.py:209
  381.6 2.4 copy.73
  384.0 4.0 all-to-all-start.3
  388.1 16.2 %fusion.8 = f32[1024,1024]{0,1:T(8,128)} fusion(f32[1024]{0:T(1024)S(1)} %select_multiply_fusion, s32[1024]{0:T(1024)S(1)} %copy-done.15), kind=kLoop, calls=%fused_computation.23 | loop fusion | flops 15728640 | bytes 4202496 | tf_op jit(solution)/shard_map/mul | solution.py:40
  404.3 8.5 %gather_fusion.3 = f32[1024,1024]{1,0:T(8,128)} fusion(f32[1024,1024]{0,1:T(8,128)} %fusion.8, s32[1024]{0:T(1024)S(1)} %broadcast_clamp_fusion), kind=kCustom, calls=%fused_computation.3 | custom fusion | bytes 8392704 | tf_op jit(solution)/shard_map/jit(_take)/gather | solution.py:173
  416.2 7.3 divide_add_fusion.1
  423.5 1.7 collective-permute-start.4
  426.7 3.5 collective-permute-start.3
  432.7 19.5 %collective-permute-done.3 = f32[256,1024]{1,0:T(8,128)S(1)} collective-permute-done((f32[256,1024]{1,0:T(8,128)S(1)}, f32[256,1024]{1,0:T(8,128)S(1)}, u32[]{:S(2)}, u32[]{:S(2)}) %collective-permute-start.3) | collective-permute-done | bytes 1048608 | tf_op jit(solution)/shard_map/ppermute | solution.py:31
  452.4 25.7 %fusion.27 = f32[2,256,1024]{2,1,0:T(8,128)} fusion(f32[2,257,1024]{2,1,0:T(8,128)S(1)} %fusion.43, f32[2,256,1024]{2,1,0:T(8,128)S(1)} %copy-done.14, f32[2,256,1024]{2,1,0:T(8,128)S(1)} %divide_add_fusion.1, f32[1,256,1024]{2,1,0:T(8,128)S(1)} %get-tuple-element.15, f32[1,256,1024]{2,1,0:T(8,128)S(1)} %select_bitcast_fusion.1, ...), kind=kOutput, calls=%fused_computation.42 | convolution fusion | flops 6461849600 | bytes 14684672 | tf_op jit(solution)/shard_map/dot_general | solution.py:46
  478.2 4.1 copy.77
  482.3 54.1 %all_to_all.134 = f32[2,256,1024]{1,0,2:T(2,128)S(1)} all-to-all(f32[2,256,1024]{1,0,2:T(2,128)} %copy.77), channel_id=1, replica_groups=mesh['tm'=8,'rows'=4] {'tm'}, dimensions={2} | all-to-all | bytes 4194304 | tf_op jit(solution)/shard_map/all_to_all | solution.py:189
  537.9 2.9 copy.79
  540.8 3.0 copy.80
  543.8 30.4 %all_to_all.135 = f32[16,256,128]{1,0,2:T(8,128)} all-to-all(f32[16,256,128]{1,0,2:T(8,128)} %copy.80), channel_id=1, replica_groups=mesh['tm'=8,'rows'=4] {'rows'}, dimensions={2} | all-to-all | bytes 4194304 | tf_op jit(solution)/shard_map/all_to_all | solution.py:188
  574.2 6.3 copy.82
  580.5 7.0 reshape.508
  587.5 6.0 dot_general.72
  593.5 6.4 copy.83
  599.9 5.0 fusion.107
  604.9 33.5 %fusion.58 = f32[2,16,1024,32]{2,3,1,0:T(8,128)S(1)} fusion(f32[2,16,1024,32]{2,1,3,0:T(8,128)S(1)} %fusion.107, s32[1024]{0:T(1024)S(1)} %copy-done.15), kind=kOutput, calls=%fused_computation.75 | convolution fusion | flops 12899581952 | bytes 8392704 | tf_op jit(solution)/shard_map/kn,afnc->afkc/dot_general | solution.py:56
  639.5 30.6 %fusion.63 = f32[2,16,1024,32]{2,3,1,0:T(8,128)} fusion(f32[1,16,1024,32]{2,3,1,0:T(8,128)S(1)} %get-tuple-element.11, f32[1,16,1024,32]{2,3,1,0:T(8,128)S(1)} %get-tuple-element.10, f32[1024]{0:T(1024)S(1)} %select_multiply_fusion, s32[1024]{0:T(1024)S(1)} %copy-done.15), kind=kOutput, calls=%fused_computation.76 | convolution fusion | flops 12901679104 | bytes 8396800 | tf_op jit(solution)/shard_map/kn,afnc->afkc/dot_general | solution.py:56
  670.2 10.4 %copy.86 = f32[2,16,1024,32]{3,2,1,0:T(8,128)} copy(f32[2,16,1024,32]{2,3,1,0:T(8,128)} %fusion.63) | data formatting | bytes 8388608 | tf_op jit(solution)/shard_map/kn,afnc->afkc/transpose | solution.py:56
  680.6 11.7 %reshape.509 = f32[32,32768]{1,0:T(8,128)} reshape(f32[2,16,1024,32]{3,2,1,0:T(8,128)} %copy.86) | data formatting | bytes 8388608 | tf_op jit(solution)/shard_map/reshape | solution.py:76
  692.4 9.8 %dot_general.77 = f32[1024,32,32]{1,0,2:T(8,128)} reshape(f32[32768,32]{0,1:T(8,128)} %bitcast.227) | data formatting | bytes 8388608 | tf_op jit(solution)/shard_map/dot_general | solution.py:75
  702.2 11.8 %copy.87 = f32[1024,32,32]{0,2,1:T(8,128)} copy(f32[1024,32,32]{1,0,2:T(8,128)} %dot_general.77) | data formatting | bytes 8388608 | tf_op jit(solution)/shard_map/dot_general | solution.py:75
  714.0 4.1 fusion.163
  719.4 51.5 %all_to_all.136 = f32[16,1024,32]{1,2,0:T(8,128)S(1)} all-to-all(f32[16,1024,32]{1,2,0:T(8,128)S(1)} %copy.88), channel_id=1, replica_groups=mesh['tm'=8,'rows'=4] {'tm'}, dimensions={0} | all-to-all | bytes 4194304 | tf_op jit(solution)/shard_map/all_to_all | solution.py:209
  772.3 4.1 copy.90
  776.4 29.5 %all_to_all.137 = f32[2,1024,256]{2,0,1:T(2,128)S(1)} all-to-all(f32[2,1024,256]{2,0,1:T(2,128)} %copy.90), channel_id=1, replica_groups=mesh['tm'=8,'rows'=4] {'rows'}, dimensions={1} | all-to-all | bytes 4194304 | tf_op jit(solution)/shard_map/all_to_all | solution.py:208
  806.3 1.9 copy-done.11
  808.2 8.6 %divide_add_fusion = f32[2,256,1024]{2,1,0:T(8,128)} fusion(f32[2,256,1024]{2,1,0:T(8,128)S(1)} %divide_add_fusion.1, f32[2]{0:T(128)S(1)} %multiply_exponential_fusion, f32[2,256,1024]{2,1,0:T(8,128)S(1)} %bitcast.264, f32[1024,1024]{1,0:T(8,128)S(1)} %copy-done.11, pred[1024]{0:T(1024)(128)(4,1)S(1)} %compare_and_fusion), kind=kOutput, calls=%fused_computation.121 | convolution fusion | flops 6444548096 | bytes 10486792 | tf_op jit(solution)/shard_map/dot_general | solution.py:46
  (137 shorter events, 54.4 us)
Async XLA Ops:
  0.0 15.9 %copy-start = (f32[8,128,128]{2,1,0:T(8,128)S(1)}, f32[8,128,128]{2,1,0:T(8,128)}, u32[]{:S(2)}) copy-start(f32[8,128,128]{2,1,0:T(8,128)} %param.8) | copy-start | bytes 1572868
  0.0 73.5 %collective-permute-start = (f32[256,1024]{1,0:T(8,128)}, f32[256,1024]{1,0:T(8,128)}, u32[]{:S(2)}, u32[]{:S(2)}) collective-permute-start(f32[256,1024]{1,0:T(8,128)} %param.6), channel_id=1, source_target_pairs={{0,4},{4,8},{8,12},{12,16},{16,20},{20,24},{24,28},{1,5},{5,9},{9,... | collective-permute-start | bytes 3145736 | tf_op jit(solution)/shard_map/ppermute | solution.py:31
  7.4 62.2 %collective-permute-start.1 = (f32[2,1,1024]{2,1,0:T(1,128)}, f32[2,1,1024]{2,1,0:T(1,128)S(1)}, u32[]{:S(2)}, u32[]{:S(2)}) collective-permute-start(f32[2,1,1024]{2,1,0:T(1,128)} %broadcast_in_dim.376), channel_id=1, source_target_pairs={{0,1},{1,2},{2,3},{4,5},{5,6},{6,7},{8,9},{9,10},{10,11},{12,13},{... | collective-permute-start | bytes 24584 | tf_op jit(solution)/shard_map/ppermute | solution.py:20
  9.4 60.1 %collective-permute-start.2 = (f32[2,1,1024]{2,1,0:T(1,128)}, f32[2,1,1024]{2,1,0:T(1,128)S(1)}, u32[]{:S(2)}, u32[]{:S(2)}) collective-permute-start(f32[2,1,1024]{2,1,0:T(1,128)} %broadcast_in_dim.377), channel_id=1, source_target_pairs={{1,0},{2,1},{3,2},{5,4},{6,5},{7,6},{9,8},{10,9},{11,10},{13,12},{... | collective-permute-start | bytes 24584 | tf_op jit(solution)/shard_map/ppermute | solution.py:23
  25.5 1.4 copy-start.2
  42.9 10.6 %copy-start.16 = (s32[258]{0:T(512)S(1)}, s32[258]{0:T(512)}, u32[]{:S(2)}) copy-start(s32[258]{0:T(512)} %fusion.170) | copy-start | bytes 3100
  42.9 10.6 %copy-start.19 = (f32[4]{0:T(128)S(1)}, f32[4]{0:T(128)}, u32[]{:S(2)}) copy-start(f32[4]{0:T(128)} %param.10) | copy-start | bytes 52
  42.9 11.2 %copy-start.18 = (f32[4]{0:T(128)S(1)}, f32[4]{0:T(128)}, u32[]{:S(2)}) copy-start(f32[4]{0:T(128)} %param.11) | copy-start | bytes 52
  42.9 11.9 %copy-start.17 = (s32[258]{0:T(512)S(1)}, s32[258]{0:T(512)}, u32[]{:S(2)}) copy-start(s32[258]{0:T(512)} %iota_add_fusion) | copy-start | bytes 3100
  43.0 11.9 %copy-start.3 = (s32[8,8]{1,0:T(8,128)S(1)}, s32[8,8]{1,0:T(8,128)}, u32[]{:S(2)}) copy-start(s32[8,8]{1,0:T(8,128)} %param.9) | copy-start | bytes 772
  45.2 10.7 %copy-start.20 = (pred[258]{0:T(512)(128)(4,1)S(1)}, pred[258]{0:T(512)(128)(4,1)}, u32[]{:S(2)}) copy-start(pred[258]{0:T(512)(128)(4,1)} %compare_and_fusion.1) | copy-start | bytes 778
  67.8 2.0 copy-start.6
  68.2 1.4 copy-start.4
  69.5 1.2 copy-start.8
  70.8 1.2 copy-start.12
  73.5 1.6 copy-start.13
  73.5 1.6 copy-start.15
  161.3 30.2 %all-to-all-start.1 = ((f32[16,256,128]{1,0,2:T(8,128)}), f32[16,256,128]{1,0,2:T(8,128)S(1)}, u32[]{:S(2)}, u32[]{:S(2)}) async-start(f32[16,256,128]{1,0,2:T(8,128)} %copy.63), calls=%async_computation.1 | async-start | bytes 4194304 | tf_op jit(solution)/shard_map/all_to_all | solution.py:188
  384.0 29.6 %all-to-all-start.3 = ((f32[2,1024,256]{2,0,1:T(2,128)}), f32[2,1024,256]{2,0,1:T(2,128)S(1)}, u32[]{:S(2)}, u32[]{:S(2)}) async-start(f32[2,1024,256]{2,0,1:T(2,128)} %copy.73), calls=%async_computation.3 | async-start | bytes 4194304 | tf_op jit(solution)/shard_map/all_to_all | solution.py:208
  413.7 2.2 copy-start.10
  413.8 2.4 copy-start.5
  423.5 6.8 copy-start.7
  423.5 6.8 copy-start.9
  423.5 6.7 collective-permute-start.4
  425.3 5.0 collective-permute-start.5
  426.7 25.5 %collective-permute-start.3 = (f32[256,1024]{1,0:T(8,128)S(1)}, f32[256,1024]{1,0:T(8,128)S(1)}, u32[]{:S(2)}, u32[]{:S(2)}) collective-permute-start(f32[256,1024]{1,0:T(8,128)S(1)} %get-tuple-element.14), channel_id=1, source_target_pairs={{0,4},{4,8},{8,12},{12,16},{16,20},{20,24},{24,28},{1,5},{5,9},{9,... | collective-permute-start | bytes 3145736 | tf_op jit(solution)/shard_map/ppermute | solution.py:31
  432.7 19.7 %copy-start.14 = (f32[2,256,1024]{2,1,0:T(8,128)S(1)}, f32[2,256,1024]{2,1,0:T(8,128)}, u32[]{:S(2)}) copy-start(f32[2,256,1024]{2,1,0:T(8,128)} %select_add_fusion) | copy-start | bytes 6291460
  806.0 2.2 copy-start.11
  808.2 8.6 %copy-start.1 = (f32[8,128,128]{2,1,0:T(8,128)S(1)}, f32[8,128,128]{2,1,0:T(8,128)}, u32[]{:S(2)}) copy-start(f32[8,128,128]{2,1,0:T(8,128)} %param.8) | copy-start | bytes 1572868
where the time goes:
time: 825 us; the launch traced here: 817 us
  blocking collectives  269 us (33%)
  local copies, waits for them, and re-layouts  224 us (27%)
  matrix products  212 us (26%)
  waiting for transfers between devices  44.3 us (5%)
  other arithmetic  42 us (5%)
  starting transfers between devices  23.8 us (3%)
    dot_general x4, matrix products, along_rows(): return jnp.einsum('kn,afnc->afkc', table, values, precision=HIGHEST)  128 us
    all_to_all x2, blocking collectives, shards(): lax.all_to_all(column_modes, 'tm', split_axis=2, concat_axis=0, tiled=True)  106 us
    all_to_all x2, blocking collectives, shards(): lax.all_to_all(field, 'tm', split_axis=0, concat_axis=2, tiled=True)  103 us
    dot_general x4, matrix products, along_last(): jnp.dot(values.reshape(-1, array_extent[-1]), table.T, precision=HIGHEST,...  67.6 us
    dot_general x6, local copies, waits for them, and re-layouts, fourier_inverse(): jnp.dot(table, values.reshape(2 * count, -1), precision=HIGHEST, preferre...  45.7 us
    all_to_all x1, blocking collectives, shards(): lax.all_to_all(lax.all_to_all(column_modes, 'tm', split_axis=2, concat_ax...  30.4 us
    all_to_all x1, blocking collectives, shards(): lax.all_to_all(lax.all_to_all(field, 'tm', split_axis=0, concat_axis=2, t...  29.5 us
    broadcast_in_dim x25, local copies, waits for them, and re-layouts, shards(): jnp.where((chosen == pattern)[..., None], pattern_rows[pattern][None, :,...  25.2 us
  transfers between devices with their start and end apart: 8, of which 3 were waited for; matrix products, arithmetic and copies ran while one was open for 11% of the time, Pallas kernels for 0%

commit v1 on v0

--- a/solution.py
+++ b/solution.py
@@ -185,13 +185,10 @@
         )
         scaled = defect_vector * amplification[:, None, None]
         column_modes = along_last(scaled, column_fwd)
-        gathered = lax.all_to_all(
-            lax.all_to_all(column_modes, "tm", split_axis=2, concat_axis=0, tiled=True),
-            "rows",
-            split_axis=2,
-            concat_axis=1,
-            tiled=True,
-        )
+        own = lax.all_to_all(column_modes, "tm", split_axis=2, concat_axis=0, tiled=True)
+        parts = jnp.split(own, lax.axis_size("rows"), axis=2)
+        incoming = lax.all_to_all(jnp.stack(parts), "rows", 0, 0)
+        gathered = jnp.concatenate(incoming, axis=1)
         column_width = gathered.shape[2]
         column_ids = (
             lax.axis_index("tm") * (rows_count * column_width)

time: 825 us -> 856 us (1.038)
  local copies, waits for them, and re-layouts: 224 us -> 252 us
    another operation x0 -> x12, local copies, waits for them, and re-layouts: none -> 45.7 us  [the longest x10 32.8 us: shards(): incoming = lax.all_to_all(jnp.stack(parts), 'rows', 0, 0)]
    all_to_all x2 -> x0, local copies, waits for them, and re-layouts: 11 us -> none  [shards(): lax.all_to_all(lax.all_to_all(column_modes, 'tm', split_axis=2, concat_ax...]
where the time goes in v1:
time: 856 us; the launch traced here: 848 us
  blocking collectives  268 us (31%)
  local copies, waits for them, and re-layouts  252 us (29%)
  matrix products  213 us (25%)
  other arithmetic  46.1 us (5%)
  waiting for transfers between devices  44.1 us (5%)
  starting transfers between devices  24 us (3%)
    dot_general x4, matrix products, along_rows(): return jnp.einsum('kn,afnc->afkc', table, values, precision=HIGHEST)  128 us
    all_to_all x2, blocking collectives, shards(): lax.all_to_all(column_modes, 'tm', split_axis=2, concat_axis=0, tiled=True)  107 us
    all_to_all x2, blocking collectives, shards(): lax.all_to_all(field, 'tm', split_axis=0, concat_axis=2, tiled=True)  103 us
    dot_general x4, matrix products, along_last(): jnp.dot(values.reshape(-1, array_extent[-1]), table.T, precision=HIGHEST,...  67.8 us
    dot_general x6, local copies, waits for them, and re-layouts, fourier_inverse(): jnp.dot(table, values.reshape(2 * count, -1), precision=HIGHEST, preferre...  45.6 us
    another operation x10, local copies, waits for them, and re-layouts, shards(): incoming = lax.all_to_all(jnp.stack(parts), 'rows', 0, 0)  32.8 us
    all_to_all x1, blocking collectives, shards(): lax.all_to_all(lax.all_to_all(field, 'tm', split_axis=0, concat_axis=2, t...  29.5 us
    all_to_all x1, blocking collectives, shards(): incoming = lax.all_to_all(jnp.stack(parts), 'rows', 0, 0)  29 us
  transfers between devices with their start and end apart: 8, of which 3 were waited for; matrix products, arithmetic and copies ran while one was open for 11% of the time, Pallas kernels for 0%

profile of v1, /device:TPU:0, one launch (start us, length us, event | category | flops | bytes accessed | tf_op | source)
XLA Modules:
  0.0 847.9 jit_solution(5942086468273990027)
XLA Ops:
  0.0 6.0 collective-permute-start
  12.5 2.9 subtract_multiply_fusion
  16.0 2.4 gather_fusion.1
  42.7 2.3 broadcast_in_dim.345
  47.0 2.2 broadcast_in_dim.351
  51.1 2.2 broadcast_in_dim.357
  55.8 2.7 select_select_fusion.1
  58.5 2.5 select_select_fusion
  61.1 5.9 select_add_fusion
  74.8 26.2 %fusion.29 = f32[2,256,1024]{2,1,0:T(8,128)} fusion(f32[2,257,1024]{2,1,0:T(8,128)S(1)} %fusion.46, f32[2,256,1024]{2,1,0:T(8,128)S(1)} %copy-done.14, f32[1,256,1024]{2,1,0:T(8,128)S(1)} %bitcast.239, f32[1,256,1024]{2,1,0:T(8,128)S(1)} %select_bitcast_fusion.2, s32[1024]{0:T(1024)S(1)} %copy-done.16, f32[2,256,1023]{2,1,0:T(8,128)S(1)} %fusion.91, ...), kind=kOutput, calls=%fused_computation.44 | convolution fusion | flops 6461849600 | bytes 13636096 | tf_op jit(solution)/shard_map/dot_general | solution.py:46
  101.0 2.8 copy.62
  103.9 52.3 %all_to_all.112 = f32[2,256,1024]{1,0,2:T(2,128)S(1)} all-to-all(f32[2,256,1024]{1,0,2:T(2,128)S(1)} %copy.62), channel_id=1, replica_groups=mesh['tm'=8,'rows'=4] {'tm'}, dimensions={2} | all-to-all | bytes 4194304 | tf_op jit(solution)/shard_map/all_to_all | solution.py:188
  159.7 5.0 slice_bitcast_fusion.7
  164.7 2.2 copy.65
  166.8 2.3 copy.66
  169.2 3.0 copy.67
  173.5 2.8 pad_maximum_fusion
  176.3 4.6 all-to-all-start.1
  182.4 24.1 %all-to-all-done.1 = f32[4,16,256,32]{2,3,1,0:T(8,128)S(1)} async-done(((f32[4,16,256,32]{2,3,1,0:T(8,128)}), f32[4,16,256,32]{2,3,1,0:T(8,128)S(1)}, u32[]{:S(2)}, u32[]{:S(2)}) %all-to-all-start.1) | async-done | bytes 2097184 | tf_op jit(solution)/shard_map/all_to_all | solution.py:190
  206.5 4.7 copy.69
  211.3 6.0 reshape_reshape.6
  217.3 4.8 dot_general.61
  222.1 5.5 copy.70
  227.6 3.4 fusion.109
  231.0 33.4 %fusion.53 = f32[2,16,1024,32]{2,3,1,0:T(8,128)S(1)} fusion(f32[2,16,1024,32]{2,1,3,0:T(8,128)S(1)} %fusion.109, s32[1024]{0:T(1024)S(1)} %copy-done.16), kind=kOutput, calls=%fused_computation.74 | convolution fusion | flops 12899581952 | bytes 8392704 | tf_op jit(solution)/shard_map/kn,afnc->afkc/dot_general | solution.py:56
  265.6 30.6 %fusion.68 = f32[2,16,1024,32]{2,3,1,0:T(8,128)} fusion(f32[1,16,1024,32]{2,3,1,0:T(8,128)S(1)} %get-tuple-element.13, f32[1,16,1024,32]{2,3,1,0:T(8,128)S(1)} %get-tuple-element.12, f32[1024]{0:T(1024)S(1)} %select_multiply_fusion, s32[1024]{0:T(1024)S(1)} %copy-done.16), kind=kOutput, calls=%fused_computation.77 | convolution fusion | flops 12901679104 | bytes 8396800 | tf_op jit(solution)/shard_map/kn,afnc->afkc/dot_general | solution.py:56
  296.2 10.5 %copy.73 = f32[2,16,1024,32]{3,2,1,0:T(8,128)} copy(f32[2,16,1024,32]{2,3,1,0:T(8,128)} %fusion.68) | data formatting | bytes 8388608 | tf_op jit(solution)/shard_map/kn,afnc->afkc/transpose | solution.py:56
  306.6 11.6 %reshape.505 = f32[32,32768]{1,0:T(8,128)} reshape(f32[2,16,1024,32]{3,2,1,0:T(8,128)} %copy.73) | data formatting | bytes 8388608 | tf_op jit(solution)/shard_map/reshape | solution.py:76
  318.3 9.9 %dot_general.66 = f32[1024,32,32]{1,0,2:T(8,128)} reshape(f32[32768,32]{0,1:T(8,128)} %bitcast.240) | data formatting | bytes 8388608 | tf_op jit(solution)/shard_map/dot_general | solution.py:75
  328.1 11.7 %copy.74 = f32[1024,32,32]{0,2,1:T(8,128)} copy(f32[1024,32,32]{1,0,2:T(8,128)} %dot_general.66) | data formatting | bytes 8388608 | tf_op jit(solution)/shard_map/dot_general | solution.py:75
  339.9 4.1 fusion.165
  345.3 51.1 %all_to_all.113 = f32[16,1024,32]{1,2,0:T(8,128)S(1)} all-to-all(f32[16,1024,32]{1,2,0:T(8,128)S(1)} %copy.75), channel_id=1, replica_groups=mesh['tm'=8,'rows'=4] {'tm'}, dimensions={0} | all-to-all | bytes 4194304 | tf_op jit(solution)/shard_map/all_to_all | solution.py:206
  396.6 2.4 copy.77
  399.0 3.8 all-to-all-start.3
  402.9 16.2 %fusion.8 = f32[1024,1024]{0,1:T(8,128)} fusion(f32[1024]{0:T(1024)S(1)} %select_multiply_fusion, s32[1024]{0:T(1024)S(1)} %copy-done.16), kind=kLoop, calls=%fused_computation.23 | loop fusion | flops 15728640 | bytes 4202496 | tf_op jit(solution)/shard_map/mul | solution.py:40
  419.1 8.6 %gather_fusion.3 = f32[1024,1024]{1,0:T(8,128)} fusion(f32[1024,1024]{0,1:T(8,128)} %fusion.8, s32[1024]{0:T(1024)S(1)} %broadcast_clamp_fusion), kind=kCustom, calls=%fused_computation.3 | custom fusion | bytes 8392704 | tf_op jit(solution)/shard_map/jit(_take)/gather | solution.py:173
  431.0 7.3 divide_add_fusion.1
  441.6 3.8 collective-permute-start.3
  447.9 19.3 %collective-permute-done.3 = f32[256,1024]{1,0:T(8,128)S(1)} collective-permute-done((f32[256,1024]{1,0:T(8,128)S(1)}, f32[256,1024]{1,0:T(8,128)S(1)}, u32[]{:S(2)}, u32[]{:S(2)}) %collective-permute-start.3) | collective-permute-done | bytes 1048608 | tf_op jit(solution)/shard_map/ppermute | solution.py:31
  467.3 25.7 %fusion.27 = f32[2,256,1024]{2,1,0:T(8,128)} fusion(f32[2,257,1024]{2,1,0:T(8,128)S(1)} %fusion.43, f32[2,256,1024]{2,1,0:T(8,128)S(1)} %copy-done.15, f32[2,256,1024]{2,1,0:T(8,128)S(1)} %divide_add_fusion.1, f32[1,256,1024]{2,1,0:T(8,128)S(1)} %get-tuple-element.19, f32[1,256,1024]{2,1,0:T(8,128)S(1)} %select_bitcast_fusion.1, ...), kind=kOutput, calls=%fused_computation.42 | convolution fusion | flops 6461849600 | bytes 14684672 | tf_op jit(solution)/shard_map/dot_general | solution.py:46
  493.1 4.1 copy.81
  497.2 54.3 %all_to_all.114 = f32[2,256,1024]{1,0,2:T(2,128)S(1)} all-to-all(f32[2,256,1024]{1,0,2:T(2,128)} %copy.81), channel_id=1, replica_groups=mesh['tm'=8,'rows'=4] {'tm'}, dimensions={2} | all-to-all | bytes 4194304 | tf_op jit(solution)/shard_map/all_to_all | solution.py:188
  553.0 2.9 copy.83
  555.9 8.7 %slice_bitcast_fusion.3 = (f32[1,16,256,32]{3,2,1,0:T(8,128)}, f32[1,16,256,32]{3,2,1,0:T(8,128)}, f32[1,16,256,32]{3,2,1,0:T(8,128)}, f32[1,16,256,32]{3,2,1,0:T(8,128)}) fusion(f32[16,256,128]{2,1,0:T(8,128)} %bitcast.238), kind=kLoop, calls=%fused_computation.90 | loop fusion | bytes 4194304 | tf_op jit(solution)/shard_map/stack | solution.py:190
  566.7 2.2 copy.85
  568.9 3.0 copy.86
  571.9 3.0 copy.87
  576.2 29.0 %all_to_all.115 = f32[4,16,256,32]{2,3,1,0:T(8,128)} all-to-all(f32[4,16,256,32]{2,3,1,0:T(8,128)S(1)} %pad_maximum_fusion.1), channel_id=1, replica_groups=mesh['tm'=8,'rows'=4] {'rows'}, dimensions={0} | all-to-all | bytes 4194304 | tf_op jit(solution)/shard_map/all_to_all | solution.py:190
  605.2 6.3 copy.88
  611.5 7.0 reshape_reshape.7
  618.4 6.0 dot_general.72
  624.5 6.4 copy.89
  630.9 5.0 fusion.107
  635.9 33.4 %fusion.58 = f32[2,16,1024,32]{2,3,1,0:T(8,128)S(1)} fusion(f32[2,16,1024,32]{2,1,3,0:T(8,128)S(1)} %fusion.107, s32[1024]{0:T(1024)S(1)} %copy-done.16), kind=kOutput, calls=%fused_computation.75 | convolution fusion | flops 12899581952 | bytes 8392704 | tf_op jit(solution)/shard_map/kn,afnc->afkc/dot_general | solution.py:56
  670.5 30.7 %fusion.63 = f32[2,16,1024,32]{2,3,1,0:T(8,128)} fusion(f32[1,16,1024,32]{2,3,1,0:T(8,128)S(1)} %get-tuple-element.11, f32[1,16,1024,32]{2,3,1,0:T(8,128)S(1)} %get-tuple-element.10, f32[1024]{0:T(1024)S(1)} %select_multiply_fusion, s32[1024]{0:T(1024)S(1)} %copy-done.16), kind=kOutput, calls=%fused_computation.76 | convolution fusion | flops 12901679104 | bytes 8396800 | tf_op jit(solution)/shard_map/kn,afnc->afkc/dot_general | solution.py:56
  701.2 10.5 %copy.92 = f32[2,16,1024,32]{3,2,1,0:T(8,128)} copy(f32[2,16,1024,32]{2,3,1,0:T(8,128)} %fusion.63) | data formatting | bytes 8388608 | tf_op jit(solution)/shard_map/kn,afnc->afkc/transpose | solution.py:56
  711.6 11.7 %reshape.507 = f32[32,32768]{1,0:T(8,128)} reshape(f32[2,16,1024,32]{3,2,1,0:T(8,128)} %copy.92) | data formatting | bytes 8388608 | tf_op jit(solution)/shard_map/reshape | solution.py:76
  723.4 9.9 %dot_general.77 = f32[1024,32,32]{1,0,2:T(8,128)} reshape(f32[32768,32]{0,1:T(8,128)} %bitcast.241) | data formatting | bytes 8388608 | tf_op jit(solution)/shard_map/dot_general | solution.py:75
  733.2 11.7 %copy.93 = f32[1024,32,32]{0,2,1:T(8,128)} copy(f32[1024,32,32]{1,0,2:T(8,128)} %dot_general.77) | data formatting | bytes 8388608 | tf_op jit(solution)/shard_map/dot_general | solution.py:75
  744.9 4.1 fusion.163
  750.3 51.4 %all_to_all.116 = f32[16,1024,32]{1,2,0:T(8,128)S(1)} all-to-all(f32[16,1024,32]{1,2,0:T(8,128)S(1)} %copy.94), channel_id=1, replica_groups=mesh['tm'=8,'rows'=4] {'tm'}, dimensions={0} | all-to-all | bytes 4194304 | tf_op jit(solution)/shard_map/all_to_all | solution.py:206
  803.2 4.1 copy.96
  807.3 29.5 %all_to_all.117 = f32[2,1024,256]{2,0,1:T(2,128)S(1)} all-to-all(f32[2,1024,256]{2,0,1:T(2,128)} %copy.96), channel_id=1, replica_groups=mesh['tm'=8,'rows'=4] {'rows'}, dimensions={1} | all-to-all | bytes 4194304 | tf_op jit(solution)/shard_map/all_to_all | solution.py:205
  839.1 8.6 %divide_add_fusion = f32[2,256,1024]{2,1,0:T(8,128)} fusion(f32[2,256,1024]{2,1,0:T(8,128)S(1)} %divide_add_fusion.1, f32[2]{0:T(128)S(1)} %multiply_exponential_fusion, f32[2,256,1024]{2,1,0:T(8,128)S(1)} %bitcast.276, f32[1024,1024]{1,0:T(8,128)S(1)} %copy-done.12, pred[1024]{0:T(1024)(128)(4,1)S(1)} %compare_and_fusion), kind=kOutput, calls=%fused_computation.131 | convolution fusion | flops 6444548096 | bytes 10486792 | tf_op jit(solution)/shard_map/dot_general | solution.py:46
  (149 shorter events, 73.9 us)
Async XLA Ops:
  0.0 16.0 %copy-start = (f32[8,128,128]{2,1,0:T(8,128)S(1)}, f32[8,128,128]{2,1,0:T(8,128)}, u32[]{:S(2)}) copy-start(f32[8,128,128]{2,1,0:T(8,128)} %param.8) | copy-start | bytes 1572868
  0.0 73.3 %collective-permute-start = (f32[256,1024]{1,0:T(8,128)}, f32[256,1024]{1,0:T(8,128)}, u32[]{:S(2)}, u32[]{:S(2)}) collective-permute-start(f32[256,1024]{1,0:T(8,128)} %param.6), channel_id=1, source_target_pairs={{0,4},{4,8},{8,12},{12,16},{16,20},{20,24},{24,28},{1,5},{5,9},{9,... | collective-permute-start | bytes 3145736 | tf_op jit(solution)/shard_map/ppermute | solution.py:31
  7.4 61.9 %collective-permute-start.1 = (f32[2,1,1024]{2,1,0:T(1,128)}, f32[2,1,1024]{2,1,0:T(1,128)S(1)}, u32[]{:S(2)}, u32[]{:S(2)}) collective-permute-start(f32[2,1,1024]{2,1,0:T(1,128)} %broadcast_in_dim.376), channel_id=1, source_target_pairs={{0,1},{1,2},{2,3},{4,5},{5,6},{6,7},{8,9},{9,10},{10,11},{12,13},{... | collective-permute-start | bytes 24584 | tf_op jit(solution)/shard_map/ppermute | solution.py:20
  9.4 59.9 %collective-permute-start.2 = (f32[2,1,1024]{2,1,0:T(1,128)}, f32[2,1,1024]{2,1,0:T(1,128)S(1)}, u32[]{:S(2)}, u32[]{:S(2)}) collective-permute-start(f32[2,1,1024]{2,1,0:T(1,128)} %broadcast_in_dim.377), channel_id=1, source_target_pairs={{1,0},{2,1},{3,2},{5,4},{6,5},{7,6},{9,8},{10,9},{11,10},{13,12},{... | collective-permute-start | bytes 24584 | tf_op jit(solution)/shard_map/ppermute | solution.py:23
  25.6 1.4 copy-start.2
  42.7 10.6 %copy-start.17 = (s32[258]{0:T(512)S(1)}, s32[258]{0:T(512)}, u32[]{:S(2)}) copy-start(s32[258]{0:T(512)} %fusion.170) | copy-start | bytes 3100
  42.7 10.6 %copy-start.20 = (f32[4]{0:T(128)S(1)}, f32[4]{0:T(128)}, u32[]{:S(2)}) copy-start(f32[4]{0:T(128)} %param.10) | copy-start | bytes 52
  42.7 11.3 %copy-start.19 = (f32[4]{0:T(128)S(1)}, f32[4]{0:T(128)}, u32[]{:S(2)}) copy-start(f32[4]{0:T(128)} %param.11) | copy-start | bytes 52
  42.7 12.0 %copy-start.18 = (s32[258]{0:T(512)S(1)}, s32[258]{0:T(512)}, u32[]{:S(2)}) copy-start(s32[258]{0:T(512)} %iota_add_fusion) | copy-start | bytes 3100
  42.7 12.0 %copy-start.3 = (s32[8,8]{1,0:T(8,128)S(1)}, s32[8,8]{1,0:T(8,128)}, u32[]{:S(2)}) copy-start(s32[8,8]{1,0:T(8,128)} %param.9) | copy-start | bytes 772
  45.0 10.8 %copy-start.21 = (pred[258]{0:T(512)(128)(4,1)S(1)}, pred[258]{0:T(512)(128)(4,1)}, u32[]{:S(2)}) copy-start(pred[258]{0:T(512)(128)(4,1)} %compare_and_fusion.1) | copy-start | bytes 778
  67.6 2.0 copy-start.6
  68.0 1.4 copy-start.4
  69.3 1.2 copy-start.8
  70.5 1.2 copy-start.13
  73.2 1.6 copy-start.14
  73.2 1.6 copy-start.16
  166.8 5.3 copy-start.10
  176.3 30.2 %all-to-all-start.1 = ((f32[4,16,256,32]{2,3,1,0:T(8,128)}), f32[4,16,256,32]{2,3,1,0:T(8,128)S(1)}, u32[]{:S(2)}, u32[]{:S(2)}) async-start(f32[4,16,256,32]{2,3,1,0:T(8,128)} %pad_maximum_fusion), calls=%async_computation.1 | async-start | bytes 4194304 | tf_op jit(solution)/shard_map/all_to_all | solution.py:190
  399.0 29.4 %all-to-all-start.3 = ((f32[2,1024,256]{2,0,1:T(2,128)}), f32[2,1024,256]{2,0,1:T(2,128)S(1)}, u32[]{:S(2)}, u32[]{:S(2)}) async-start(f32[2,1024,256]{2,0,1:T(2,128)} %copy.77), calls=%async_computation.3 | async-start | bytes 4194304 | tf_op jit(solution)/shard_map/all_to_all | solution.py:205
  428.5 2.2 copy-start.11
  428.6 2.4 copy-start.5
  438.3 7.1 copy-start.7
  438.3 7.1 copy-start.9
  438.4 7.0 collective-permute-start.4
  440.1 5.2 collective-permute-start.5
  441.6 25.5 %collective-permute-start.3 = (f32[256,1024]{1,0:T(8,128)S(1)}, f32[256,1024]{1,0:T(8,128)S(1)}, u32[]{:S(2)}, u32[]{:S(2)}) collective-permute-start(f32[256,1024]{1,0:T(8,128)S(1)} %get-tuple-element.18), channel_id=1, source_target_pairs={{0,4},{4,8},{8,12},{12,16},{16,20},{20,24},{24,28},{1,5},{5,9},{9,... | collective-permute-start | bytes 3145736 | tf_op jit(solution)/shard_map/ppermute | solution.py:31
  447.8 19.5 %copy-start.15 = (f32[2,256,1024]{2,1,0:T(8,128)S(1)}, f32[2,256,1024]{2,1,0:T(8,128)}, u32[]{:S(2)}) copy-start(f32[2,256,1024]{2,1,0:T(8,128)} %select_add_fusion) | copy-start | bytes 6291460
  836.9 2.2 copy-start.12
  839.1 8.6 %copy-start.1 = (f32[8,128,128]{2,1,0:T(8,128)S(1)}, f32[8,128,128]{2,1,0:T(8,128)}, u32[]{:S(2)}) copy-start(f32[8,128,128]{2,1,0:T(8,128)} %param.8) | copy-start | bytes 1572868
